TPU v7x, 128 devices: a whole 4x4x4 slice. The times are simulated.
128 devices in a mesh: curve: 8 (over x, core), group: 16 (over y, z).
Axes of the slice: x: 4, y: 4, z: 4, core: 2. Of those that a mesh axis runs over, the one named last changes fastest.
Arguments:
- composition: float32 [6144, 53, 256], P(('curve', 'group')), may hold values from -4 to 4
- heat_level: float32 [6144, 256], P(('curve', 'group')), may hold values from 1000 to 2500
- step_counts: int32 [6144], P(('curve', 'group')), may hold values from 1 to 3
- burning_parcel_roster: int32 [768], P(('curve', 'group')), may hold values from 0 to 47, as said below
- target_compute_place: int32 [768], P(('curve', 'group')), may hold values from -1 to 383, as said below
- partial_reciprocal_operator: float32 [768, 53, 53], P(('curve', 'group')), may hold values from -0.03 to 0.13
- speed_log_prefactor: float32 [268], replicated, may hold values from -1 to 1
- arrhenius_barrier: float32 [268], replicated, may hold values from 0.5 to 4
- leading_ingredient: float32 [268, 53], replicated, may hold values from -0.875 to 0.875
- trailing_ingredient: float32 [268, 53], replicated, may hold values from -0.875 to 0.875
- molar_coefficients: float32 [53, 268], replicated, may hold values from -0.375 to 0.375
Outputs:
- new_species: float32 [6144, 53, 256], P(('curve', 'group'))
Inputs may be any that keep to these rules, and one draw needn't show every extreme that they name: `burning_parcel_roster`: each owner's 6 entries name distinct blocks among its own 48 blocks. `target_compute_place`: -1 marks an entry that does not react; an owner's reacting entries come first in its list, and an owner has 0 to 6 of them. A value g sends the block to compute slot g % 3 of device g // 3, devices numbered with curve slowest; that device has the owner's curve index. Every value 0 to 383 appears exactly once, so each device integrates exactly 3 blocks; one owner sends at most 1 block to one device, and in every curve row some owner has 6 reacting entries and some owner has none.
All inputs are finite; a program needn't handle non-finite values.
Results may differ from a plain program's by a relative error of at most 0.0003.
Values sent between devices are 32-bit elements; how exact they have to be, the bound alone decides.
No kernel may reach another device: no remote copies, remote signals or barrier semaphores. Data moves between devices by JAX's collectives and lax.ppermute only.
A program may use at most 64 MiB of HBM per device.

v0:
```python
import jax
import jax.numpy as jnp
from jax import lax
from jax.sharding import PartitionSpec as P

SUBS = 3
MAXIN = 3


step_size = 0.2
section_shift = (2.0, 1.92, 0.24)
section_couple = (-8.0, 14.88, 2.4, -0.896, -0.432, -0.4)
section_weight = (19.0 / 9.0, 0.5, 25.0 / 108.0, 125.0 / 108.0)


def in_one_piece(arrays, axis, split_dim, concat_dim, along):
    columns = [a.reshape(*a.shape[:along], -1) for a in arrays]
    both = jnp.concatenate(columns, axis=along)
    result, at, finished = (
        lax.all_to_all(both, axis, split_axis=split_dim, concat_axis=concat_dim, tiled=True),
        0,
        [],
    )
    for a, column in zip(arrays, columns):
        piece = result[..., at : at + column.shape[along]]
        finished.append(piece.reshape(*piece.shape[:along], *a.shape[along:]))
        at += column.shape[along]
    return tuple(finished)


def kinetic_speed_coefficients(heat_level, speed_log_prefactor, arrhenius_barrier):
    reciprocal_operator = 1000.0 / heat_level
    return jnp.exp(
        speed_log_prefactor[None, :, None]
        - arrhenius_barrier[None, :, None] * (reciprocal_operator[:, None, :] - 0.6)
    )


def net_rates(present_composition, kinetic_speed_coefficient, reactants, molar_coefficients):
    paired = jnp.einsum(
        "rs,msc->mrc", reactants, present_composition, precision=lax.Precision.HIGHEST
    )
    reaction_count = kinetic_speed_coefficient.shape[1]
    progress = kinetic_speed_coefficient * paired[:, :reaction_count] * paired[:, reaction_count:]
    return jnp.einsum("sr,mrc->msc", molar_coefficients, progress, precision=lax.Precision.HIGHEST)


def apply_matrix(matrix, vector):
    return jnp.einsum("mst,mtc->msc", matrix, vector, precision=lax.Precision.HIGHEST)


def advance_partial_step(
    present_composition,
    heat_level,
    step_counts,
    partial_reciprocal_operator,
    speed_log_prefactor,
    arrhenius_barrier,
    leading_ingredient,
    trailing_ingredient,
    molar_coefficients,
):
    reactants = jnp.concatenate([leading_ingredient, trailing_ingredient], axis=0)
    kinetic_speed_coefficient = kinetic_speed_coefficients(
        heat_level, speed_log_prefactor, arrhenius_barrier
    )
    weights = step_counts.astype(jnp.float32)
    per_step = (weights / step_size)[:, None, None]
    scaled = partial_reciprocal_operator / weights[:, None, None]
    for substep in range(SUBS):
        rates_one = net_rates(
            present_composition, kinetic_speed_coefficient, reactants, molar_coefficients
        )
        section_one = apply_matrix(scaled, rates_one)
        point_two = present_composition + section_shift[0] * section_one
        rates_two = net_rates(point_two, kinetic_speed_coefficient, reactants, molar_coefficients)
        section_two = apply_matrix(scaled, rates_two + section_couple[0] * per_step * section_one)
        point_three = (
            present_composition + section_shift[1] * section_one + section_shift[2] * section_two
        )
        rates_three = net_rates(
            point_three, kinetic_speed_coefficient, reactants, molar_coefficients
        )
        section_three = apply_matrix(
            scaled,
            rates_three
            + per_step * (section_couple[1] * section_one + section_couple[2] * section_two),
        )
        section_four = apply_matrix(
            scaled,
            rates_three
            + per_step
            * (
                section_couple[3] * section_one
                + section_couple[4] * section_two
                + section_couple[5] * section_three
            ),
        )
        advanced = (
            present_composition
            + section_weight[0] * section_one
            + section_weight[1] * section_two
            + section_weight[2] * section_three
            + section_weight[3] * section_four
        )
        active = (substep < step_counts)[:, None, None]
        present_composition = jnp.where(active, advanced, present_composition)
    return present_composition


def on_device(
    composition,
    heat_level,
    step_counts,
    burning_parcel_roster,
    target_compute_place,
    partial_reciprocal_operator,
    speed_log_prefactor,
    arrhenius_barrier,
    leading_ingredient,
    trailing_ingredient,
    molar_coefficients,
):
    members = lax.axis_size("group")
    listed = burning_parcel_roster.shape[0]
    capacity = (listed + members - 1) // members
    outgoing = members * capacity
    reacts = target_compute_place >= 0
    target = jnp.where(reacts, target_compute_place // MAXIN % members, -1)
    position = jnp.arange(listed, dtype=jnp.int32)
    earlier = (
        (target[:, None] == target[None, :])
        & reacts[None, :]
        & (position[None, :] < position[:, None])
    )
    ranking = jnp.sum(earlier.astype(jnp.int32), axis=1)
    buffer_pos = target * capacity + ranking
    slot_index = jnp.arange(outgoing, dtype=jnp.int32)
    matches = (buffer_pos[None, :] == slot_index[:, None]) & reacts[None, :]
    chosen = jnp.sum(jnp.where(matches, position[None, :] + 1, 0), axis=1) - 1
    occupied_places = chosen >= 0
    entry_index = jnp.maximum(chosen, 0)
    line_placement_number = burning_parcel_roster[entry_index]
    filled_weight = occupied_places.astype(jnp.float32)
    send_species = composition[line_placement_number] * filled_weight[:, None, None]
    departing_heat_level = jnp.where(
        occupied_places[:, None], heat_level[line_placement_number], 1000.0
    )
    send_matrix = partial_reciprocal_operator[entry_index] * filled_weight[:, None, None]
    local_slot = jnp.where(occupied_places, target_compute_place[entry_index] % MAXIN, 0)
    send_meta = jnp.stack(
        [
            step_counts[line_placement_number].astype(jnp.float32),
            local_slot.astype(jnp.float32),
            filled_weight,
        ],
        axis=1,
    )
    landed_items = in_one_piece(
        (send_species, departing_heat_level, send_matrix, send_meta), "group", 0, 0, 1
    )
    incoming_composition, incoming_heat_level, incoming_operator, incoming_metadata = landed_items
    got_weight = incoming_metadata[:, 0]
    got_local = incoming_metadata[:, 1].astype(jnp.int32)
    got_live = incoming_metadata[:, 2] > 0.5
    compute_index = jnp.arange(MAXIN, dtype=jnp.int32)
    pairing = (got_local[None, :] == compute_index[:, None]) & got_live[None, :]
    sending_holder = jnp.maximum(
        jnp.sum(jnp.where(pairing, slot_index[None, :] + 1, 0), axis=1) - 1, 0
    )
    advanced = advance_partial_step(
        incoming_composition[sending_holder],
        incoming_heat_level[sending_holder],
        got_weight[sending_holder].astype(jnp.int32),
        incoming_operator[sending_holder],
        speed_log_prefactor,
        arrhenius_barrier,
        leading_ingredient,
        trailing_ingredient,
        molar_coefficients,
    )
    finished = (
        advanced[jnp.clip(got_local, 0, MAXIN - 1)] * got_live.astype(jnp.float32)[:, None, None]
    )
    returned = lax.all_to_all(finished, "group", split_axis=0, concat_axis=0, tiled=True)
    block_index = jnp.arange(composition.shape[0], dtype=jnp.int32)
    owned = (burning_parcel_roster[None, :] == block_index[:, None]) & reacts[None, :]
    picked = jnp.sum(jnp.where(owned, buffer_pos[None, :] + 1, 0), axis=1) - 1
    return jnp.where((picked >= 0)[:, None, None], returned[jnp.maximum(picked, 0)], composition)


def solution(mesh):
    return jax.shard_map(
        on_device,
        mesh=mesh,
        in_specs=(
            P(("curve", "group"), None, None),
            P(("curve", "group"), None),
            P(("curve", "group")),
            P(("curve", "group")),
            P(("curve", "group")),
            P(("curve", "group"), None, None),
            P(),
            P(),
            P(),
            P(),
            P(),
        ),
        out_specs=P(("curve", "group"), None, None),
        check_vma=False,
    )
```

profile of v0, /device:TPU:0, one launch (start us, length us, event | category | flops | bytes accessed | tf_op | source)
XLA Modules:
  0.0 119.9 jit_solution(17764788329928825741)
XLA Ops:
  8.4 2.7 %gather_fusion.1 = f32[16,53,256]{2,0,1:T(8,128)} fusion(f32[48,53,256]{2,0,1:T(8,128)S(1)} %copy-done.2, s32[1024]{0:T(1024)S(1)} %pad_clamp_fusion.3), kind=kCustom, calls=%fused_computation.1 | custom fusion | bytes 1736768 | tf_op jit(solution)/shard_map/gather | solution.py:145
  13.5 2.1 %concatenate.6 = f32[16,16636]{1,0:T(8,128)} concatenate(f32[16,13568]{1,0:T(8,128)} %broadcast_multiply_fusion.1, f32[16,256]{1,0:T(8,128)S(1)} %broadcast_select_fusion, f32[16,2809]{1,0:T(8,128)S(1)} %broadcast_multiply_fusion.2, f32[16,1]{1,0:T(8,128)S(1)} %copy.75, f32[16,1]{1,0:T(8,128)S(1)} %fusion.136, f32[16,1]{1,0:T(8,128)S(1)} %copy.76), dimensions={1} | concatenate | bytes 2129408 | tf_op jit(solution)/shard_map/concatenate | solution.py:18
  15.6 3.4 %copy.77 = f32[16,1,16636]{2,1,0:T(1,128)} copy(f32[16,1,16636]{2,0,1:T(8,128)} %bitcast.95) | data formatting | bytes 2129408 | tf_op jit(solution)/shard_map/all_to_all | solution.py:20
  18.9 8.4 %all-to-all-start = ((f32[16,1,16636]{2,1,0:T(1,128)}), f32[16,1,16636]{2,1,0:T(1,128)}, u32[]{:S(2)}, u32[]{:S(2)}) async-start(f32[16,1,16636]{2,1,0:T(1,128)} %copy.77), calls=%async_computation | async-start | bytes 2129920 | tf_op jit(solution)/shard_map/all_to_all | solution.py:20
  27.3 17.8 %all-to-all-done = f32[16,1,16636]{2,1,0:T(1,128)} async-done(((f32[16,1,16636]{2,1,0:T(1,128)}), f32[16,1,16636]{2,1,0:T(1,128)}, u32[]{:S(2)}, u32[]{:S(2)}) %all-to-all-start) | async-done | bytes 1064736 | tf_op jit(solution)/shard_map/all_to_all | solution.py:20
  50.1 2.1 %slice.127 = f32[16,13568]{1,0:T(8,128)} slice(f32[16,16636]{1,0:T(8,128)} %bitcast.94), slice={[0:16], [0:13568]} | slice | bytes 1736704 | tf_op jit(solution)/shard_map/slice | solution.py:25
  52.8 2.2 %reshape.195 = f32[16,53,256]{2,1,0:T(8,128)} reshape(f32[16,13568]{1,0:T(8,128)} %slice.127) | data formatting | bytes 1736704 | tf_op jit(solution)/shard_map/reshape | solution.py:26
  55.0 1.8 %gather_fusion.7 = f32[3,53,256]{2,1,0:T(8,128)S(1)} fusion(f32[16,53,256]{2,1,0:T(8,128)} %reshape.195, s32[1024]{0:T(1024)S(1)} %pad_clamp_fusion.2), kind=kCustom, calls=%fused_computation.7 | custom fusion | bytes 325644 | tf_op jit(solution)/shard_map/gather | solution.py:172
  59.4 1.6 %convolution_bitcast_fusion.8 = f32[3,536,256]{2,1,0:T(8,128)S(1)} fusion(f32[3,53,256]{2,1,0:T(8,128)S(1)} %gather_fusion.7, f32[268,53]{0,1:T(8,128)S(1)} %copy-done.3, f32[268,53]{0,1:T(8,128)S(1)} %copy-done.4), kind=kOutput, calls=%fused_computation.21 | convolution fusion | flops 261836544 | bytes 1923040 | tf_op jit(solution)/shard_map/rs,msc->mrc/dot_general | solution.py:40
  61.0 1.9 %fusion.11 = f32[3,256,53]{1,2,0:T(8,128)S(1)} fusion(f32[3,536,256]{2,1,0:T(8,128)S(1)} %convolution_bitcast_fusion.8, f32[3,256]{1,0:T(4,128)S(1)} %divide_add_fusion, f32[268]{0:T(512)S(1)} %copy-done.8, f32[268]{0:T(512)S(1)} %copy-done.9, f32[53,268]{1,0:T(8,128)} %param.21), kind=kOutput, calls=%fused_computation.60 | convolution fusion | flops 131727360 | bytes 1898992 | tf_op jit(solution)/shard_map/sr,mrc->msc/dot_general | solution.py:45
  63.3 1.6 %convolution_bitcast_fusion.7 = f32[3,536,256]{2,1,0:T(8,128)S(1)} fusion(f32[3,53,256]{2,1,0:T(8,128)S(1)} %gather_fusion.7, f32[3,53,256]{2,1,0:T(8,128)S(1)} %fusion.178, f32[268,53]{0,1:T(8,128)S(1)} %copy-done.3, f32[268,53]{0,1:T(8,128)S(1)} %copy-done.4), kind=kOutput, calls=%fused_computation.20 | convolution fusion | flops 261917952 | bytes 2085856 | tf_op jit(solution)/shard_map/rs,msc->mrc/dot_general | solution.py:40
  66.3 1.6 %convolution_bitcast_fusion.6 = f32[3,536,256]{2,1,0:T(8,128)S(1)} fusion(f32[3,53,256]{2,1,0:T(8,128)S(1)} %fusion.177, f32[3,53,256]{2,1,0:T(8,128)S(1)} %gather_fusion.7, f32[3,53,256]{2,1,0:T(8,128)S(1)} %fusion.178, f32[268,53]{0,1:T(8,128)S(1)} %copy-done.3, f32[268,53]{0,1:T(8,128)S(1)} %copy-done.4), kind=kOutput, calls=%fused_computation.19 | convolution fusion | flops 261999360 | bytes 2248672 | tf_op jit(solution)/shard_map/rs,msc->mrc/dot_general | solution.py:40
  69.6 1.6 %convolution_bitcast_fusion.5 = f32[3,536,256]{2,1,0:T(8,128)S(1)} fusion(f32[3,53,256]{2,1,0:T(8,128)S(1)} %fusion.8, f32[268,53]{0,1:T(8,128)S(1)} %copy-done.3, f32[268,53]{0,1:T(8,128)S(1)} %copy-done.4), kind=kOutput, calls=%fused_computation.18 | convolution fusion | flops 261836544 | bytes 1923040 | tf_op jit(solution)/shard_map/rs,msc->mrc/dot_general | solution.py:40
  72.6 1.8 %convolution_bitcast_fusion.4 = f32[3,536,256]{2,1,0:T(8,128)S(1)} fusion(f32[3,53,256]{2,1,0:T(8,128)S(1)} %fusion.8, f32[3,53,256]{2,1,0:T(8,128)S(1)} %fusion.176, f32[268,53]{0,1:T(8,128)S(1)} %copy-done.3, f32[268,53]{0,1:T(8,128)S(1)} %copy-done.4), kind=kOutput, calls=%fused_computation.17 | convolution fusion | flops 261917952 | bytes 2085856 | tf_op jit(solution)/shard_map/rs,msc->mrc/dot_general | solution.py:40
  75.8 1.6 %convolution_bitcast_fusion.3 = f32[3,536,256]{2,1,0:T(8,128)S(1)} fusion(f32[3,53,256]{2,1,0:T(8,128)S(1)} %fusion.175, f32[3,53,256]{2,1,0:T(8,128)S(1)} %fusion.8, f32[3,53,256]{2,1,0:T(8,128)S(1)} %fusion.176, f32[268,53]{0,1:T(8,128)S(1)} %copy-done.3, f32[268,53]{0,1:T(8,128)S(1)} %copy-done.4), kind=kOutput, calls=%fused_computation.16 | convolution fusion | flops 261999360 | bytes 2248672 | tf_op jit(solution)/shard_map/rs,msc->mrc/dot_general | solution.py:40
  79.2 1.6 %convolution_bitcast_fusion.2 = f32[3,536,256]{2,1,0:T(8,128)S(1)} fusion(f32[3,53,256]{2,1,0:T(8,128)S(1)} %fusion.6, f32[268,53]{0,1:T(8,128)S(1)} %copy-done.3, f32[268,53]{0,1:T(8,128)S(1)} %copy-done.4), kind=kOutput, calls=%fused_computation.15 | convolution fusion | flops 261836544 | bytes 1923040 | tf_op jit(solution)/shard_map/rs,msc->mrc/dot_general | solution.py:40
  82.1 1.6 %convolution_bitcast_fusion.1 = f32[3,536,256]{2,1,0:T(8,128)S(1)} fusion(f32[3,53,256]{2,1,0:T(8,128)S(1)} %fusion.6, f32[3,53,256]{2,1,0:T(8,128)S(1)} %fusion.174, f32[268,53]{0,1:T(8,128)S(1)} %copy-done.3, f32[268,53]{0,1:T(8,128)S(1)} %copy-done.4), kind=kOutput, calls=%fused_computation.14 | convolution fusion | flops 261917952 | bytes 2085856 | tf_op jit(solution)/shard_map/rs,msc->mrc/dot_general | solution.py:40
  85.1 1.6 %convolution_bitcast_fusion = f32[3,536,256]{2,1,0:T(8,128)S(1)} fusion(f32[3,53,256]{2,1,0:T(8,128)S(1)} %fusion.173, f32[3,53,256]{2,1,0:T(8,128)S(1)} %fusion.6, f32[3,53,256]{2,1,0:T(8,128)S(1)} %fusion.174, f32[268,53]{0,1:T(8,128)S(1)} %copy-done.3, f32[268,53]{0,1:T(8,128)S(1)} %copy-done.4), kind=kOutput, calls=%fused_computation.13 | convolution fusion | flops 261999360 | bytes 2248672 | tf_op jit(solution)/shard_map/rs,msc->mrc/dot_general | solution.py:40
  90.3 2.2 %broadcast_multiply_fusion = f32[16,53,256]{2,1,0:T(8,128)} fusion(f32[16,53,256]{2,1,0:T(8,128)} %gather_fusion.10, f32[16]{0:T(128)S(1)} %convert_element_type.105), kind=kLoop, calls=%fused_computation.63 | loop fusion | flops 217088 | bytes 1736768 | tf_op jit(solution)/shard_map/mul | solution.py:183
  92.5 4.3 %all-to-all-start.1 = ((f32[16,53,256]{2,1,0:T(8,128)}), f32[16,53,256]{2,1,0:T(8,128)}, u32[]{:S(2)}, u32[]{:S(2)}) async-start(f32[16,53,256]{2,1,0:T(8,128)} %broadcast_multiply_fusion), calls=%async_computation.1 | async-start | bytes 1835008 | tf_op jit(solution)/shard_map/all_to_all | solution.py:185
  97.0 13.5 %all-to-all-done.1 = f32[16,53,256]{2,1,0:T(8,128)} async-done(((f32[16,53,256]{2,1,0:T(8,128)}), f32[16,53,256]{2,1,0:T(8,128)}, u32[]{:S(2)}, u32[]{:S(2)}) %all-to-all-start.1) | async-done | bytes 868384 | tf_op jit(solution)/shard_map/all_to_all | solution.py:185
  110.5 3.5 %gather_fusion.11 = f32[48,53,256]{2,1,0:T(8,128)} fusion(f32[16,53,256]{2,1,0:T(8,128)} %all-to-all-done.1, s32[1024]{0:T(1024)S(1)} %pad_clamp_fusion), kind=kCustom, calls=%fused_computation.11 | custom fusion | bytes 5210304 | tf_op jit(solution)/shard_map/gather | solution.py:189
  113.9 3.6 %copy_select_fusion = f32[48,53,256]{2,1,0:T(8,128)S(1)} fusion(f32[48,53,256]{2,1,0:T(8,128)} %gather_fusion.11, f32[48,53,256]{2,0,1:T(8,128)S(1)} %copy-done.2, pred[48]{0:T(512)(128)(4,1)S(1)} %add_compare_fusion.1), kind=kLoop, calls=%fused_computation.12 | loop fusion | flops 651264 | bytes 7815216 | tf_op jit(solution)/shard_map/jit(_where)/select_n | solution.py:189
  117.6 2.3 %copy.79 = f32[48,53,256]{2,0,1:T(8,128)} copy(f32[48,53,256]{2,1,0:T(8,128)S(1)} %copy_select_fusion) | data formatting | bytes 5210112 | tf_op jit(solution)/shard_map/jit(_where)/select_n | solution.py:189
  (92 shorter events, 33.1 us)
Async XLA Ops:
  0.0 7.7 %copy-start = (f32[6,53,53]{2,1,0:T(8,128)S(1)}, f32[6,53,53]{2,1,0:T(8,128)}, u32[]{:S(2)}) copy-start(f32[6,53,53]{2,1,0:T(8,128)} %param.16) | copy-start | bytes 202252
  0.0 7.1 %copy-start.6 = (f32[48,256]{1,0:T(8,128)S(1)}, f32[48,256]{1,0:T(8,128)}, u32[]{:S(2)}) copy-start(f32[48,256]{1,0:T(8,128)} %param.12) | copy-start | bytes 147460
  2.5 6.0 %copy-start.2 = (f32[48,53,256]{2,0,1:T(8,128)S(1)}, f32[48,53,256]{2,0,1:T(8,128)}, u32[]{:S(2)}) copy-start(f32[48,53,256]{2,0,1:T(8,128)} %param.11) | copy-start | bytes 7815172
  18.9 26.2 %all-to-all-start = ((f32[16,1,16636]{2,1,0:T(1,128)}), f32[16,1,16636]{2,1,0:T(1,128)}, u32[]{:S(2)}, u32[]{:S(2)}) async-start(f32[16,1,16636]{2,1,0:T(1,128)} %copy.77), calls=%async_computation | async-start | bytes 2129920 | tf_op jit(solution)/shard_map/all_to_all | solution.py:20
  46.5 1.0 copy-start.5
  52.2 7.1 %copy-start.3 = (f32[268,53]{0,1:T(8,128)S(1)}, f32[268,53]{0,1:T(8,128)}, u32[]{:S(2)}) copy-start(f32[268,53]{0,1:T(8,128)} %param.20) | copy-start | bytes 170452
  52.2 7.1 %copy-start.4 = (f32[268,53]{0,1:T(8,128)S(1)}, f32[268,53]{0,1:T(8,128)}, u32[]{:S(2)}) copy-start(f32[268,53]{0,1:T(8,128)} %param.19) | copy-start | bytes 170452
  55.0 6.0 %copy-start.8 = (f32[268]{0:T(512)S(1)}, f32[268]{0:T(512)}, u32[]{:S(2)}) copy-start(f32[268]{0:T(512)} %param.18) | copy-start | bytes 3220
  55.0 6.0 %copy-start.9 = (f32[268]{0:T(512)S(1)}, f32[268]{0:T(512)}, u32[]{:S(2)}) copy-start(f32[268]{0:T(512)} %param.17) | copy-start | bytes 3220
  62.9 2.0 %copy-start.7 = (f32[53,268]{1,0:T(8,128)S(1)}, f32[53,268]{1,0:T(8,128)}, u32[]{:S(2)}) copy-start(f32[53,268]{1,0:T(8,128)} %param.21) | copy-start | bytes 170452
  90.3 6.6 %copy-start.1 = (s32[6]{0:T(128)S(1)}, s32[6]{0:T(128)}, u32[]{:S(2)}) copy-start(s32[6]{0:T(128)} %param.14) | copy-start | bytes 76
  92.5 17.9 %all-to-all-start.1 = ((f32[16,53,256]{2,1,0:T(8,128)}), f32[16,53,256]{2,1,0:T(8,128)}, u32[]{:S(2)}, u32[]{:S(2)}) async-start(f32[16,53,256]{2,1,0:T(8,128)} %broadcast_multiply_fusion), calls=%async_computation.1 | async-start | bytes 1835008 | tf_op jit(solution)/shard_map/all_to_all | solution.py:185
where the time goes:
time: 121 us; the launch traced here: 120 us
  local copies, waits for them, and re-layouts  36.1 us (30%)
  waiting for transfers between devices  31.3 us (26%)
  matrix products  29.1 us (24%)
  starting transfers between devices  12.7 us (10%)
  other arithmetic  10.2 us (8%)
    all_to_all x1, waiting for transfers between devices, in_one_piece(): lax.all_to_all(both, axis, split_axis=split_dim, concat_axis=concat_dim,...  17.8 us
    dot_general x9, matrix products, net_rates(): jnp.einsum('rs,msc->mrc', reactants, present_composition, precision=lax.P...  14.6 us
    all_to_all x1, waiting for transfers between devices, on_device(): lax.all_to_all(finished, 'group', split_axis=0, concat_axis=0, tiled=True)  13.5 us
    dot_general x9, matrix products, net_rates(): jnp.einsum('sr,mrc->msc', molar_coefficients, progress, precision=lax.Pre...  10.2 us
    all_to_all x1, starting transfers between devices, in_one_piece(): lax.all_to_all(both, axis, split_axis=split_dim, concat_axis=concat_dim,...  8.39 us
    dot_general x12, matrix products, apply_matrix(): jnp.einsum('mst,mtc->msc', matrix, vector, precision=lax.Precision.HIGHEST)  4.33 us
    all_to_all x1, starting transfers between devices, on_device(): lax.all_to_all(finished, 'group', split_axis=0, concat_axis=0, tiled=True)  4.31 us
    gather x2, local copies, waits for them, and re-layouts, on_device(): composition[line_placement_number] * filled_weight[:, None, None]  3.88 us
  transfers between devices with their start and end apart: 2, of which 2 were waited for; matrix products, arithmetic and copies ran while one was open for 0% of the time, Pallas kernels for 0%

commit v1 on v0

v1 whole, which is shorter than its diff:
```python
import functools

import jax
import jax.numpy as jnp
from jax import lax
from jax.experimental import pallas as pl
from jax.experimental.pallas import tpu as pltpu
from jax.sharding import PartitionSpec as P

SUBS = 3
STREAMS = 3

SHIFT_B1 = 1.92
SHIFT_B2 = 0.24
G1_A = (25.0 * 14.88 - 125.0 * 0.896) / 108.0
G1_AA = -(50.0 * 14.88) / 108.0
G2_A = (25.0 * 2.4 - 125.0 * 0.432) / 108.0
G2_AA = -(50.0 * 2.4) / 108.0

F32 = jnp.float32
BF16 = jnp.bfloat16


def dot(a, b):
    return jnp.dot(a, b, preferred_element_type=F32)


def halves(x):
    high = x.astype(BF16).astype(F32)
    return high, x - high


def tall(x):
    high = x.astype(BF16)
    low = (x - high.astype(F32)).astype(BF16)
    return jnp.concatenate([high, low, high], axis=0)


def wide(x):
    high, low = halves(x)
    first = high + pltpu.roll(high, 64, 1)
    return jnp.concatenate([first.astype(BF16), low.astype(BF16)], axis=1)


def after_rest(rest, x):
    rest_high, rest_low = halves(rest)
    high, low = halves(x)
    left = rest_high + pltpu.roll(rest_high, 16, 1) + pltpu.roll(rest_low, 32, 1)
    left = left + pltpu.roll(high, 64, 1)
    right = high + pltpu.roll(low, 64, 1)
    return jnp.concatenate([left.astype(BF16), right.astype(BF16)], axis=1)


def column(row, count):
    square = jnp.broadcast_to(row, (128, row.shape[1]))
    return square.T[:count]


def body(
    listed, species, reactions, cells,
    comp, heat, steps, roster, target, operator, prefactor, barrier, lead, trail, molar,
    out,
    block, heat_v, op_v, pre_v, bar_v, lead_v, trail_v, molar_v,
    steps_s, roster_s, target_s, tasks,
    y_s, kf_s, reactants_f, reactants_w, op_f, molar_f, molar_t,
    mc_s, mcrest_s, d3_s, r2_s, r3_s, e1_s,
    sems, block_sems, out_sems,
):
    copies = [
        pltpu.make_async_copy(src, dst, sems.at[i])
        for i, (src, dst) in enumerate(
            [
                (roster, roster_s),
                (steps, steps_s),
                (target, target_s),
                (operator, op_v),
                (molar, molar_v),
                (lead, lead_v),
                (trail, trail_v),
                (heat, heat_v),
                (prefactor, pre_v),
                (barrier, bar_v),
            ]
        )
    ]
    for copy in copies:
        copy.start()
    whole = pltpu.make_async_copy(comp, out, sems.at[len(copies)])

    y_s[...] = jnp.zeros_like(y_s)
    reactants_f[...] = jnp.zeros_like(reactants_f)
    op_f[...] = jnp.zeros_like(op_f)
    molar_f[...] = jnp.zeros_like(molar_f)

    for copy in copies[:3]:
        copy.wait()
    places = [roster_s[e] for e in range(listed)]
    fetches = [
        pltpu.make_async_copy(comp.at[places[e]], block.at[e], block_sems.at[e])
        for e in range(listed)
    ]
    for fetch in fetches:
        fetch.start()
    whole.start()

    counts = [steps_s[places[e]] for e in range(listed)]
    total = jnp.int32(0)
    longest = jnp.int32(0)
    for e in range(listed):
        todo = jnp.where(target_s[e] >= 0, jnp.minimum(counts[e], SUBS), 0)
        for s in range(SUBS):
            tasks[total + s] = jnp.int32(e)
        total = total + todo
        longest = jnp.maximum(longest, todo)
    length = jnp.maximum(lax.div(total + (STREAMS - 1), jnp.int32(STREAMS)), longest)
    for s in range(STREAMS * SUBS):
        tasks[total + s] = jnp.int32(listed)

    for copy in copies[3:]:
        copy.wait()

    half = reactants_f.shape[0] // 2
    reactants_f[0:reactions, 0:species] = lead_v[...]
    reactants_f[half:half + reactions, 0:species] = trail_v[...]
    molar_f[0:species, 0:reactions] = molar_v[...]
    reactants_w[...] = wide(reactants_f[...])
    molar_t[...] = tall(molar_f[...])
    lanes = molar_f.shape[1]
    pad = jnp.zeros((1, lanes - reactions), F32)
    pre_c = column(jnp.concatenate([pre_v[...].reshape(1, reactions), pad], axis=1), half)
    bar_c = column(jnp.concatenate([bar_v[...].reshape(1, reactions), pad], axis=1), half)

    rows = lax.broadcasted_iota(jnp.int32, (64, 128), 0)
    cols = lax.broadcasted_iota(jnp.int32, (64, 128), 1)
    eye = jnp.where(rows == cols, 1.0, 0.0).astype(F32)

    for e in range(listed):
        op_f[e, 0:species, 0:species] = op_v[e]
    for e in range(listed):
        m = op_f[e]
        weight = counts[e].astype(F32)
        square = dot(wide(m)[:, :192], tall(m))
        both = dot(
            jnp.concatenate([wide(m / weight), wide(square * 5.0 / weight)], axis=0)[:, :192],
            molar_t[...],
        )
        mc = both[0:64]
        d3 = (150.0 / 108.0) * mc - (50.0 / 108.0) * both[64:128]
        for store, value in ((mc_s, mc), (d3_s, d3)):
            high, low = halves(value[:, 0:256])
            store[e, 0:64] = high.astype(BF16)
            store[e, 64:128] = low.astype(BF16)
        a = 5.0 * m
        aa = 25.0 * square
        nothing = jnp.zeros((64, 128), F32)
        mcrest_s[e] = after_rest(mc[:, 256:384], nothing)[:, 0:128]
        r2_s[e] = after_rest(mc[:, 256:384], -8.0 * a)
        r3_s[e] = after_rest(d3[:, 256:384], 0.5 * eye + G2_A * a + G2_AA * aa)
        e1_s[e] = wide((19.0 / 9.0) * eye + G1_A * a + G1_AA * aa)

    for e in range(listed):
        inverse = 1000.0 / heat_v[pl.ds(places[e], 1), :] - 0.6
        for side in range(cells // 128):
            part = slice(side * 128, side * 128 + 128)
            kf_s[e, :, part] = jnp.exp(pre_c - bar_c * inverse[:, part])
    for e in range(listed):
        fetches[e].wait()
        y_s[e, 0:species] = block[e]

    def progress(stacked, e):
        paired = dot(reactants_w[:, 0:192], stacked)
        value = kf_s[e] * paired[0:half] * paired[half:2 * half]
        high = value.astype(BF16)
        low = (value - high.astype(F32)).astype(BF16)
        rest = jnp.concatenate(
            [high[256:half], low[256:half], high[256:half], jnp.zeros((16, cells), BF16)], axis=0
        )
        return high[0:256], low[0:256], rest

    def main(store, e, high, low):
        first = dot(store[e], high)
        return first[0:64] + first[64:128] + dot(store[e, 0:64], low)

    def iteration(it, carry):
        slots = [tasks[k * length + it] for k in range(STREAMS)]
        mats = [jnp.minimum(q, listed - 1) for q in slots]
        ks = range(STREAMS)
        y = [y_s[slots[k]] for k in ks]
        p = [progress(tall(y[k]), mats[k]) for k in ks]
        g1 = [main(mc_s, mats[k], p[k][0], p[k][1]) + dot(mcrest_s[mats[k], :, 0:64], p[k][2]) for k in ks]
        t1 = [tall(g1[k]) for k in ks]
        p = [progress(tall(y[k] + 2.0 * g1[k]), mats[k]) for k in ks]
        g2 = [
            main(mc_s, mats[k], p[k][0], p[k][1])
            + dot(r2_s[mats[k]], jnp.concatenate([p[k][2], t1[k]], axis=0))
            for k in ks
        ]
        y3 = [y[k] + SHIFT_B1 * g1[k] + SHIFT_B2 * g2[k] for k in ks]
        p = [progress(tall(y3[k]), mats[k]) for k in ks]
        last = [
            y[k]
            + dot(e1_s[mats[k], :, 0:192], t1[k])
            + main(d3_s, mats[k], p[k][0], p[k][1])
            + dot(r3_s[mats[k]], jnp.concatenate([p[k][2], tall(g2[k])], axis=0))
            for k in ks
        ]
        for k in ks:
            y_s[slots[k]] = last[k]
        return carry

    lax.fori_loop(0, length, iteration, jnp.int32(0))

    for e in range(listed):
        block[e] = y_s[e, 0:species]
    whole.wait()
    writes = [
        pltpu.make_async_copy(block.at[e], out.at[places[e]], out_sems.at[e])
        for e in range(listed)
    ]
    for write in writes:
        write.start()
    for write in writes:
        write.wait()


def on_device(comp, heat, steps, roster, target, operator, prefactor, barrier, lead, trail, molar):
    blocks, species, cells = comp.shape
    reactions = prefactor.shape[0]
    listed = roster.shape[0]
    half = (reactions + 15) // 16 * 16
    wide_lanes = 384
    hbm = pl.BlockSpec(memory_space=pltpu.HBM)
    kernel = functools.partial(body, listed, species, reactions, cells)
    vmem = pltpu.VMEM
    return pl.pallas_call(
        kernel,
        out_shape=jax.ShapeDtypeStruct(comp.shape, comp.dtype),
        in_specs=[hbm] * 11,
        out_specs=hbm,
        scratch_shapes=[
            vmem((listed, species, cells), F32),
            vmem(heat.shape, F32),
            vmem(operator.shape, F32),
            vmem(prefactor.shape, F32),
            vmem(barrier.shape, F32),
            vmem(lead.shape, F32),
            vmem(trail.shape, F32),
            vmem(molar.shape, F32),
            pltpu.SMEM(steps.shape, jnp.int32),
            pltpu.SMEM(roster.shape, jnp.int32),
            pltpu.SMEM(target.shape, jnp.int32),
            pltpu.SMEM((listed * SUBS + STREAMS * SUBS + 8,), jnp.int32),
            vmem((listed + 1, 64, cells), F32),
            vmem((listed, half, cells), F32),
            vmem((2 * half, 128), F32),
            vmem((2 * half, 256), BF16),
            vmem((listed, 64, 128), F32),
            vmem((64, wide_lanes), F32),
            vmem((192, wide_lanes), BF16),
            vmem((listed, 128, 256), BF16),
            vmem((listed, 64, 128), BF16),
            vmem((listed, 128, 256), BF16),
            vmem((listed, 64, 256), BF16),
            vmem((listed, 64, 256), BF16),
            vmem((listed, 64, 256), BF16),
            pltpu.SemaphoreType.DMA((11,)),
            pltpu.SemaphoreType.DMA((listed,)),
            pltpu.SemaphoreType.DMA((listed,)),
        ],
        name="integrate",
    )(comp, heat, steps, roster, target, operator, prefactor, barrier, lead, trail, molar)


def solution(mesh):
    owned = ("curve", "group")
    return jax.shard_map(
        on_device,
        mesh=mesh,
        in_specs=(
            P(owned, None, None),
            P(owned, None),
            P(owned),
            P(owned),
            P(owned),
            P(owned, None, None),
            P(),
            P(),
            P(),
            P(),
            P(),
        ),
        out_specs=P(owned, None, None),
        check_vma=False,
    )
```

time: 121 us -> 98.7 us (0.82)
  Pallas kernels: 0 us -> 86.1 us
  waiting for transfers between devices: 31.3 us -> 0 us
  matrix products: 29.1 us -> 0 us
  local copies, waits for them, and re-layouts: 36.1 us -> 12.3 us
  starting transfers between devices: 12.7 us -> 0 us
  other arithmetic: 10.2 us -> 0 us
    pallas_call x0 -> x1, Pallas kernels: none -> 86.1 us  [on_device(): pl.pallas_call(kernel, out_shape=jax.ShapeDtypeStruct(comp.shape, comp.dt...]
    all_to_all x2 -> x0, waiting for transfers between devices: 31.3 us -> none  [the longest x1 17.8 us: in_one_piece(): lax.all_to_all(both, axis, split_axis=split_dim, concat_axis=concat_dim,...]
    dot_general x30 -> x0, matrix products: 29.1 us -> none  [the longest x9 14.6 us: net_rates(): jnp.einsum('rs,msc->mrc', reactants, present_composition, precision=lax.P...]
    gather x15 -> x0, local copies, waits for them, and re-layouts: 18.9 us -> none  [the longest x2 3.88 us: on_device(): composition[line_placement_number] * filled_weight[:, None, None]]
    all_to_all x2 -> x0, starting transfers between devices: 12.7 us -> none  [the longest x1 8.39 us: in_one_piece(): lax.all_to_all(both, axis, split_axis=split_dim, concat_axis=concat_dim,...]
    unnamed x21 -> x3, local copies, waits for them, and re-layouts: 1.94 us -> 8.15 us
    select_n x5 -> x0, other arithmetic: 4.69 us -> none  [the longest x1 3.64 us: on_device(): jnp.where((picked >= 0)[:, None, None], returned[jnp.maximum(picked, 0)],...]
    pallas_call x0 -> x1, local copies, waits for them, and re-layouts: none -> 4.1 us  [on_device(): pl.pallas_call(kernel, out_shape=jax.ShapeDtypeStruct(comp.shape, comp.dt...]
  transfers between devices with their start and end apart: 2 -> 0, of which waited for: 2 -> 0; matrix products, arithmetic and copies ran while one was open for 0% -> 0% of each run, Pallas kernels for 0% -> 0%
where the time goes in v1:
time: 98.7 us; the launch traced here: 98.4 us
  Pallas kernels  86.1 us (87%)
  local copies, waits for them, and re-layouts  12.3 us (12%)
    pallas_call x1, Pallas kernels, on_device(): pl.pallas_call(kernel, out_shape=jax.ShapeDtypeStruct(comp.shape, comp.dt...  86.1 us
    unnamed x3, local copies, waits for them, and re-layouts  8.15 us
    pallas_call x1, local copies, waits for them, and re-layouts, on_device(): pl.pallas_call(kernel, out_shape=jax.ShapeDtypeStruct(comp.shape, comp.dt...  4.1 us

profile of v1, /device:TPU:0, one launch (start us, length us, event | category | flops | bytes accessed | tf_op | source)
XLA Modules:
  0.0 98.4 jit_solution(3220781246100878979)
XLA Ops:
  0.0 1.7 %copy.13.lead = f32[268,53]{1,0:T(8,128)} copy(f32[268,53]{0,1:T(8,128)} %param.19) | data formatting | bytes 113632 | tf_op args[8]
  1.7 1.7 %copy.14.trail = f32[268,53]{1,0:T(8,128)} copy(f32[268,53]{0,1:T(8,128)} %param.20) | data formatting | bytes 113632 | tf_op args[9]
  3.3 4.8 %copy.12.comp = f32[48,53,256]{2,1,0:T(8,128)} copy(f32[48,53,256]{2,0,1:T(8,128)} %param.11) | data formatting | bytes 5210112 | tf_op args[0]
  8.2 86.1 %integrate.1 = f32[48,53,256]{2,1,0:T(8,128)} custom-call(f32[48,53,256]{2,1,0:T(8,128)} %copy.12.comp, f32[48,256]{1,0:T(8,128)} %heat.1, s32[48]{0:T(128)} %steps.1, s32[6]{0:T(128)} %roster.1, s32[6]{0:T(128)} %target.1, f32[6,53,53]{2,1,0:T(8,128)} %operator.1, f32[268]{0:T(512)} %prefactor.1, f32[268]{0:T(512)} %barrier.1, f32[268,53]{1,0:T(8,128)} %copy.13.lead, ...), custom_call_target="tpu_custom_call" | custom-call | tf_op jit(solution)/shard_map/integrate/pallas_call | solution.py:235
  94.3 4.1 %copy.15 = f32[48,53,256]{2,0,1:T(8,128)} copy(f32[48,53,256]{2,1,0:T(8,128)} %integrate.1) | data formatting | bytes 5210112 | tf_op jit(solution)/shard_map/integrate/pallas_call | solution.py:235
